TPU v7x, 32 devices: a whole 2x2x4 slice. The times are simulated.
32 devices in a mesh: blk: 8 (over z, x), rows: 4 (over y, core).
Axes of the slice: x: 2, y: 2, z: 4, core: 2. Of those that a mesh axis runs over, the one named last changes fastest.
Arguments:
- centers: int32 [512, 1], P(('blk', 'rows')), may hold values from 0 to 127, as said below
- gates_used: int32 [512], P(('blk', 'rows')), may hold values from 12 to 40
- jacobian: bfloat16 [512, 3, 40, 256], P(('blk', 'rows')), may hold values from -0.3984375 to 0.3984375
- weights: bfloat16 [512, 40], P(('blk', 'rows')), may hold values from 0.099609375 to 1
Outputs:
- hessian_band: float32 [128, 3, 256, 256], P(('blk', 'rows'))
Inputs may be any that keep to these rules, and one draw needn't show every extreme that they name: `centers`: cell block c is owned by blk index c // 16. Among the soundings of one device at most 4 are centred on blocks of one owner, and some owner gets exactly 4 of them; the number a device sends to the owner k places further along blk (cyclically) is the same for all devices of one rows index. Among the soundings of all devices of one rows index at most 2 share a centre block, and some block has exactly 2.
All inputs are finite; a program needn't handle non-finite values.
Results may differ from a plain program's by a relative error of at most 0.0024.
Values may be sent and summed in bfloat16 or wider, within the bound.
No kernel may reach another device: no remote copies, remote signals or barrier semaphores. Data moves between devices by JAX's collectives and lax.ppermute only.
A program may use at most 128 MiB of HBM per device.

v0:
```python
import jax
import jax.numpy as jnp
from jax import lax
from jax.sharding import PartitionSpec as P

KB = 16


def with_halo(block, sides, width):
    for axis, dim in sides:
        count = lax.axis_size(axis)
        forward = [(i, i + 1) for i in range(count - 1)]
        backward = [(target, source) for source, target in forward]
        low = lax.ppermute(
            lax.slice_in_dim(block, block.shape[dim] - width, None, axis=dim), axis, forward
        )
        high = lax.ppermute(lax.slice_in_dim(block, 0, width, axis=dim), axis, backward)
        block = jnp.concatenate([low, block, high], axis=dim)
    return block


def rank_among(labels):
    positions = jnp.arange(labels.shape[0], dtype=jnp.int32)
    before = (labels[None, :] == labels[:, None]) & (positions[None, :] < positions[:, None])
    return jnp.sum(before.astype(jnp.int32), axis=1)


def band_terms(buckets, bucket_wts, base, total_blocks):
    block_num, slot_len, foot_len, gate_len, cell_len = buckets.shape
    grid_pos = (
        base
        + jnp.arange(block_num, dtype=jnp.int32)[:, None]
        + jnp.arange(foot_len, dtype=jnp.int32)[None, :]
        - 1
    )
    inside = ((grid_pos >= 0) & (grid_pos < total_blocks)).astype(jnp.float32)
    scaled = (
        buckets.astype(jnp.float32)
        * bucket_wts.astype(jnp.float32)[:, :, None, :, None]
        * inside[:, None, :, None, None]
    ).astype(jnp.bfloat16)
    masked = buckets * inside.astype(jnp.bfloat16)[:, None, :, None, None]
    accum = jnp.zeros((block_num + 2, foot_len, cell_len, cell_len), jnp.float32)
    for lead_pos in range(foot_len):
        left = scaled[:, :, lead_pos].reshape(block_num, slot_len * gate_len, cell_len)
        for offset in range(foot_len - lead_pos):
            right = masked[:, :, lead_pos + offset].reshape(
                block_num, slot_len * gate_len, cell_len
            )
            term = lax.dot_general(
                left, right, (((1,), (1,)), ((0,), (0,))), preferred_element_type=jnp.float32
            )
            accum = accum.at[lead_pos : lead_pos + block_num, offset].add(term)
    return accum


def edge_rows(accum):
    return jnp.stack([accum[0], accum[accum.shape[0] - 1]])


def attach(accum, padded):
    block_num = accum.shape[0] - 2
    core = accum[1 : block_num + 1]
    core = core.at[0].add(padded[0])
    return core.at[block_num - 1].add(padded[3])


def on_device(centers, gates_used, jacobian, weights):
    blk_count = lax.axis_size("blk")
    sound_count, foot_len, gate_len, cell_len = jacobian.shape
    capacity = max(2, 2 * sound_count // blk_count)
    bucket_cap = max(2, 2 * sound_count // KB)
    slot_count = blk_count * capacity
    total_blocks = blk_count * KB
    centre_ids = centers[:, 0]
    owner = centre_ids // KB
    within = centre_ids - owner * KB
    order_in = rank_among(owner)
    gate_live = jnp.arange(gate_len, dtype=jnp.int32)[None, :] < gates_used[:, None]
    weight_live = jnp.where(gate_live, weights, jnp.zeros_like(weights))
    target = owner * capacity + order_in
    select = (target[None, :] == jnp.arange(slot_count, dtype=jnp.int32)[:, None]).astype(
        jnp.bfloat16
    )
    packed = (
        jnp.dot(select, jacobian.reshape(sound_count, -1), preferred_element_type=jnp.float32)
        .astype(jnp.bfloat16)
        .reshape(slot_count, foot_len, gate_len, cell_len)
    )
    packed_wts = jnp.dot(select, weight_live, preferred_element_type=jnp.float32).astype(
        jnp.bfloat16
    )
    packed_ids = jnp.dot(
        select, (within + 1).astype(jnp.bfloat16)[:, None], preferred_element_type=jnp.float32
    ).astype(jnp.bfloat16)[:, 0]
    received, received_wts, received_ids = (
        lax.all_to_all(packed, "blk", split_axis=0, concat_axis=0, tiled=True),
        lax.all_to_all(packed_wts, "blk", split_axis=0, concat_axis=0, tiled=True),
        lax.all_to_all(packed_ids, "blk", split_axis=0, concat_axis=0, tiled=True),
    )
    arrived_ids = received_ids.astype(jnp.int32)
    arrived_rank = rank_among(arrived_ids)
    bucket_target = jnp.where(arrived_ids > 0, (arrived_ids - 1) * bucket_cap + arrived_rank, -1)
    bucket_count = KB * bucket_cap
    bucket_sel = (
        bucket_target[None, :] == jnp.arange(bucket_count, dtype=jnp.int32)[:, None]
    ).astype(jnp.bfloat16)
    buckets = (
        jnp.dot(bucket_sel, received.reshape(slot_count, -1), preferred_element_type=jnp.float32)
        .astype(jnp.bfloat16)
        .reshape(KB, bucket_cap, foot_len, gate_len, cell_len)
    )
    bucket_wts = (
        jnp.dot(bucket_sel, received_wts, preferred_element_type=jnp.float32)
        .astype(jnp.bfloat16)
        .reshape(KB, bucket_cap, gate_len)
    )
    mine_blk = lax.axis_index("blk")
    share = KB // lax.axis_size("rows")
    moved, moved_wts = (
        lax.all_to_all(buckets, "rows", split_axis=0, concat_axis=1, tiled=True),
        lax.all_to_all(bucket_wts, "rows", split_axis=0, concat_axis=1, tiled=True),
    )
    base = mine_blk * KB + lax.axis_index("rows") * share
    accum = band_terms(moved, moved_wts, base, total_blocks)
    padded = with_halo(edge_rows(accum), ((("blk", "rows"), 0),), 1)
    return attach(accum, padded)


def solution(mesh):
    placed = (
        P(("blk", "rows"), None),
        P(("blk", "rows")),
        P(("blk", "rows"), None, None, None),
        P(("blk", "rows"), None),
    )
    return jax.shard_map(
        on_device,
        mesh=mesh,
        in_specs=placed,
        out_specs=P(("blk", "rows"), None, None, None),
        check_vma=False,
    )
```

profile of v0, /device:TPU:3, one launch (start us, length us, event | category | flops | bytes accessed | tf_op | source)
XLA Modules:
  0.0 140.4 jit_solution(17639520557241093231)
XLA Ops:
  0.0 0.7 and_select_fusion.1
  0.7 0.7 fusion.55
  1.5 0.7 multiply_add_fusion
  2.2 0.8 fusion.9
  3.0 0.7 all_to_all.48
  3.6 5.8 %all-to-all-start = ((bf16[8,4,1]{1,2,0:T(2,128)(2,1)}), bf16[8,4,1]{1,2,0:T(2,128)(2,1)S(1)}, u32[]{:S(2)}, u32[]{:S(2)}) async-start(bf16[8,4,1]{1,2,0:T(2,128)(2,1)} %all_to_all.48), calls=%async_computation | async-start | bytes 8192 | tf_op jit(solution)/shard_map/all_to_all | solution.py:99
  9.4 1.5 %convolution_convert_fusion.3 = bf16[32,40]{1,0:T(8,128)(2,1)} fusion(s32[16]{0:T(128)S(1)} %multiply_add_fusion, bf16[16,40]{1,0:T(8,128)(2,1)} %param.23, s32[16]{0:T(128)} %param.21), kind=kOutput, calls=%fused_computation.21 | convolution fusion | flops 44032 | bytes 3968 | tf_op jit(solution)/shard_map/dot_general | solution.py:90
  10.9 1.4 copy.23
  12.3 1.2 all-to-all-done
  13.5 4.4 %all-to-all-start.3 = ((bf16[8,4,40]{2,1,0:T(4,128)(2,1)}), bf16[8,4,40]{2,1,0:T(4,128)(2,1)S(1)}, u32[]{:S(2)}, u32[]{:S(2)}) async-start(bf16[8,4,40]{2,1,0:T(4,128)(2,1)} %bitcast.7), calls=%async_computation.3 | async-start | bytes 16384 | tf_op jit(solution)/shard_map/all_to_all | solution.py:98
  17.9 0.6 convolution_convert_fusion.1
  18.6 1.7 %copy.24 = bf16[4,8,120,256]{3,2,1,0:T(8,128)(2,1)} copy(bf16[4,8,120,256]{3,1,2,0:T(8,128)(2,1)S(1)} %bitcast.109) | data formatting | bytes 3932160
  20.2 1.9 %all-to-all-done.3 = bf16[8,4,40]{2,1,0:T(4,128)(2,1)S(1)} async-done(((bf16[8,4,40]{2,1,0:T(4,128)(2,1)}), bf16[8,4,40]{2,1,0:T(4,128)(2,1)S(1)}, u32[]{:S(2)}, u32[]{:S(2)}) %all-to-all-start.3) | async-done | bytes 2592 | tf_op jit(solution)/shard_map/all_to_all | solution.py:98
  22.1 4.7 %all-to-all-start.1 = ((bf16[32,3,40,256]{3,2,1,0:T(8,128)(2,1)}), bf16[32,3,40,256]{3,2,1,0:T(8,128)(2,1)S(1)}, u32[]{:S(2)}, u32[]{:S(2)}) async-start(bf16[32,3,40,256]{3,2,1,0:T(8,128)(2,1)} %bitcast.108), calls=%async_computation.1 | async-start | bytes 3932160 | tf_op jit(solution)/shard_map/all_to_all | solution.py:97
  27.2 0.7 reshape.492
  27.9 43.5 %all-to-all-done.1 = bf16[32,3,40,256]{3,2,1,0:T(8,128)(2,1)S(1)} async-done(((bf16[32,3,40,256]{3,2,1,0:T(8,128)(2,1)}), bf16[32,3,40,256]{3,2,1,0:T(8,128)(2,1)S(1)}, u32[]{:S(2)}, u32[]{:S(2)}) %all-to-all-start.1) | async-done | bytes 1966112 | tf_op jit(solution)/shard_map/all_to_all | solution.py:97
  71.5 4.7 %all-to-all-start.4 = ((bf16[4,2,160]{2,1,0:T(2,128)(2,1)}), bf16[4,2,160]{2,1,0:T(2,128)(2,1)S(1)}, u32[]{:S(2)}, u32[]{:S(2)}) async-start(bf16[4,2,160]{2,1,0:T(2,128)(2,1)} %reshape.492), calls=%async_computation.4 | async-start | bytes 8192 | tf_op jit(solution)/shard_map/all_to_all | solution.py:122
  76.5 0.7 convolution_convert_fusion
  77.2 1.7 %copy.26 = bf16[4,8,120,256]{3,2,1,0:T(8,128)(2,1)} copy(bf16[4,8,120,256]{3,1,2,0:T(8,128)(2,1)S(1)} %bitcast.111) | data formatting | bytes 3932160
  79.2 4.3 %all-to-all-start.2 = ((bf16[16,2,3,40,256]{4,3,2,1,0:T(8,128)(2,1)}), bf16[16,2,3,40,256]{4,3,2,1,0:T(8,128)(2,1)S(1)}, u32[]{:S(2)}, u32[]{:S(2)}) async-start(bf16[16,2,3,40,256]{4,3,2,1,0:T(8,128)(2,1)} %bitcast.42), calls=%async_computation.2 | async-start | bytes 3932160 | tf_op jit(solution)/shard_map/all_to_all | solution.py:121
  84.1 0.6 fusion.37
  84.7 0.8 and_reduce_fusion
  85.6 21.2 %all-to-all-done.2 = bf16[16,2,3,40,256]{4,3,2,1,0:T(8,128)(2,1)S(1)} async-done(((bf16[16,2,3,40,256]{4,3,2,1,0:T(8,128)(2,1)}), bf16[16,2,3,40,256]{4,3,2,1,0:T(8,128)(2,1)S(1)}, u32[]{:S(2)}, u32[]{:S(2)}) %all-to-all-start.2) | async-done | bytes 1966112 | tf_op jit(solution)/shard_map/all_to_all | solution.py:121
  109.0 1.7 %fusion.1 = f32[6,3,256,256]{3,2,0,1:T(8,128)S(1)} fusion(f32[6,3,256,256]{3,2,0,1:T(8,128)S(1)} %scatter-add.26, s32[]{:T(128)} %bitcast.16, s32[]{:T(128)} %bitcast.17, bf16[4,320,256]{2,1,0:T(8,128)(2,1)S(1)} %bitcast.101, bf16[4,320,256]{2,1,0:T(8,128)(2,1)S(1)} %bitcast.114, f32[4,1,256,256]{3,2,0,1:T(8,128)S(1)} %convolution_bitcast_fusion.5), kind=kOutput, calls=%fused_computation.12 | convolution fusion | flops 168034304 | bytes 3407880 | tf_op jit(solution)/shard_map/dot_general | solution.py:50
  110.7 2.4 %fusion.8 = f32[6,3,256,256]{3,2,0,1:T(8,128)S(1)} fusion(f32[6,3,256,256]{3,2,0,1:T(8,128)S(1)} %fusion.1, s32[]{:T(128)} %bitcast.20, s32[]{:T(128)} %bitcast.21, bf16[4,320,256]{2,1,0:T(8,128)(2,1)S(1)} %bitcast.102, bf16[4,320,256]{2,1,0:T(8,128)(2,1)S(1)} %bitcast.103, pred[]{:T(512)} %and_reduce_fusion), kind=kOutput, calls=%fused_computation.19 | convolution fusion | flops 168296448 | bytes 3407881 | tf_op jit(solution)/shard_map/dot_general | solution.py:50
  113.2 0.6 fusion.3
  114.4 0.6 fusion.7
  115.2 2.9 %collective-permute-start = (f32[1,3,256,256]{3,2,0,1:T(8,128)S(1)}, f32[1,3,256,256]{3,2,0,1:T(8,128)S(1)}, u32[]{:S(2)}, u32[]{:S(2)}) collective-permute-start(f32[1,3,256,256]{3,2,0,1:T(8,128)S(1)} %get-tuple-element.102), channel_id=1, source_target_pairs={{0,1},{1,2},{2,3},{3,4},{4,5},{5,6},{6,7},{7,8},{8,9},{9,10},{10,1... | collective-permute-start | bytes 2359304 | tf_op jit(solution)/shard_map/ppermute | solution.py:14
  118.1 1.9 %collective-permute-start.1 = (f32[1,3,256,256]{3,2,0,1:T(8,128)S(1)}, f32[1,3,256,256]{3,2,0,1:T(8,128)S(1)}, u32[]{:S(2)}, u32[]{:S(2)}) collective-permute-start(f32[1,3,256,256]{3,2,0,1:T(8,128)S(1)} %get-tuple-element.101), channel_id=1, source_target_pairs={{1,0},{2,1},{3,2},{4,3},{5,4},{6,5},{7,6},{8,7},{9,8},{10,9},{11,1... | collective-permute-start | bytes 2359304 | tf_op jit(solution)/shard_map/ppermute | solution.py:17
  120.3 15.2 %collective-permute-done = f32[1,3,256,256]{3,2,0,1:T(8,128)S(1)} collective-permute-done((f32[1,3,256,256]{3,2,0,1:T(8,128)S(1)}, f32[1,3,256,256]{3,2,0,1:T(8,128)S(1)}, u32[]{:S(2)}, u32[]{:S(2)}) %collective-permute-start) | collective-permute-done | bytes 786464 | tf_op jit(solution)/shard_map/ppermute | solution.py:14
  135.6 2.6 %collective-permute-done.1 = f32[1,3,256,256]{3,2,0,1:T(8,128)S(1)} collective-permute-done((f32[1,3,256,256]{3,2,0,1:T(8,128)S(1)}, f32[1,3,256,256]{3,2,0,1:T(8,128)S(1)}, u32[]{:S(2)}, u32[]{:S(2)}) %collective-permute-start.1) | collective-permute-done | bytes 786464 | tf_op jit(solution)/shard_map/ppermute | solution.py:17
  138.3 2.1 %copy.22 = f32[4,3,256,256]{3,2,1,0:T(8,128)} copy(f32[4,3,256,256]{3,2,0,1:T(8,128)S(1)} %fusion.10) | data formatting | bytes 6291456 | tf_op jit(solution)/shard_map/scatter-add | solution.py:65
  (31 shorter events, 5.5 us)
Async XLA Ops:
  3.6 9.9 %all-to-all-start = ((bf16[8,4,1]{1,2,0:T(2,128)(2,1)}), bf16[8,4,1]{1,2,0:T(2,128)(2,1)S(1)}, u32[]{:S(2)}, u32[]{:S(2)}) async-start(bf16[8,4,1]{1,2,0:T(2,128)(2,1)} %all_to_all.48), calls=%async_computation | async-start | bytes 8192 | tf_op jit(solution)/shard_map/all_to_all | solution.py:99
  13.5 8.6 %all-to-all-start.3 = ((bf16[8,4,40]{2,1,0:T(4,128)(2,1)}), bf16[8,4,40]{2,1,0:T(4,128)(2,1)S(1)}, u32[]{:S(2)}, u32[]{:S(2)}) async-start(bf16[8,4,40]{2,1,0:T(4,128)(2,1)} %bitcast.7), calls=%async_computation.3 | async-start | bytes 16384 | tf_op jit(solution)/shard_map/all_to_all | solution.py:98
  22.1 49.3 %all-to-all-start.1 = ((bf16[32,3,40,256]{3,2,1,0:T(8,128)(2,1)}), bf16[32,3,40,256]{3,2,1,0:T(8,128)(2,1)S(1)}, u32[]{:S(2)}, u32[]{:S(2)}) async-start(bf16[32,3,40,256]{3,2,1,0:T(8,128)(2,1)} %bitcast.108), calls=%async_computation.1 | async-start | bytes 3932160 | tf_op jit(solution)/shard_map/all_to_all | solution.py:97
  71.5 7.8 %all-to-all-start.4 = ((bf16[4,2,160]{2,1,0:T(2,128)(2,1)}), bf16[4,2,160]{2,1,0:T(2,128)(2,1)S(1)}, u32[]{:S(2)}, u32[]{:S(2)}) async-start(bf16[4,2,160]{2,1,0:T(2,128)(2,1)} %reshape.492), calls=%async_computation.4 | async-start | bytes 8192 | tf_op jit(solution)/shard_map/all_to_all | solution.py:122
  77.2 7.5 %copy-start = (s32[4]{0:T(128)S(1)}, s32[4]{0:T(128)}, u32[]{:S(2)}) copy-start(s32[4]{0:T(128)} %constant.269.clone.1) | copy-start | bytes 52
  79.2 27.6 %all-to-all-start.2 = ((bf16[16,2,3,40,256]{4,3,2,1,0:T(8,128)(2,1)}), bf16[16,2,3,40,256]{4,3,2,1,0:T(8,128)(2,1)S(1)}, u32[]{:S(2)}, u32[]{:S(2)}) async-start(bf16[16,2,3,40,256]{4,3,2,1,0:T(8,128)(2,1)} %bitcast.42), calls=%async_computation.2 | async-start | bytes 3932160 | tf_op jit(solution)/shard_map/all_to_all | solution.py:121
  115.2 20.2 %collective-permute-start = (f32[1,3,256,256]{3,2,0,1:T(8,128)S(1)}, f32[1,3,256,256]{3,2,0,1:T(8,128)S(1)}, u32[]{:S(2)}, u32[]{:S(2)}) collective-permute-start(f32[1,3,256,256]{3,2,0,1:T(8,128)S(1)} %get-tuple-element.102), channel_id=1, source_target_pairs={{0,1},{1,2},{2,3},{3,4},{4,5},{5,6},{6,7},{7,8},{8,9},{9,10},{10,1... | collective-permute-start | bytes 2359304 | tf_op jit(solution)/shard_map/ppermute | solution.py:14
  118.1 20.0 %collective-permute-start.1 = (f32[1,3,256,256]{3,2,0,1:T(8,128)S(1)}, f32[1,3,256,256]{3,2,0,1:T(8,128)S(1)}, u32[]{:S(2)}, u32[]{:S(2)}) collective-permute-start(f32[1,3,256,256]{3,2,0,1:T(8,128)S(1)} %get-tuple-element.101), channel_id=1, source_target_pairs={{1,0},{2,1},{3,2},{4,3},{5,4},{6,5},{7,6},{8,7},{9,8},{10,9},{11,1... | collective-permute-start | bytes 2359304 | tf_op jit(solution)/shard_map/ppermute | solution.py:17
where the time goes:
time: 141 us; the launch traced here: 140 us
  waiting for transfers between devices  86 us (61%)
  starting transfers between devices  28.6 us (20%)
  local copies, waits for them, and re-layouts  11.3 us (8%)
  matrix products  10.2 us (7%)
  other arithmetic  4.17 us (3%)
    all_to_all x1, waiting for transfers between devices, on_device(): lax.all_to_all(packed, 'blk', split_axis=0, concat_axis=0, tiled=True)  43.5 us
    all_to_all x1, waiting for transfers between devices, on_device(): lax.all_to_all(buckets, 'rows', split_axis=0, concat_axis=1, tiled=True)  21.2 us
    ppermute x1, waiting for transfers between devices, with_halo(): lax.ppermute(lax.slice_in_dim(block, block.shape[dim] - width, None, axis...  15.2 us
    dot_general x6, matrix products, band_terms(): lax.dot_general(left, right, (((1,), (1,)), ((0,), (0,))), preferred_elem...  6.5 us
    unnamed x8, local copies, waits for them, and re-layouts  5.87 us
    all_to_all x1, starting transfers between devices, on_device(): lax.all_to_all(packed_ids, 'blk', split_axis=0, concat_axis=0, tiled=True)  5.78 us
    all_to_all x1, starting transfers between devices, on_device(): lax.all_to_all(packed, 'blk', split_axis=0, concat_axis=0, tiled=True)  4.71 us
    all_to_all x1, starting transfers between devices, on_device(): lax.all_to_all(bucket_wts, 'rows', split_axis=0, concat_axis=1, tiled=True)  4.67 us
  transfers between devices with their start and end apart: 7, of which 7 were waited for; matrix products, arithmetic and copies ran while one was open for 8% of the time, Pallas kernels for 0%

commit v1 on v0

--- a/solution.py
+++ b/solution.py
@@ -4,6 +4,18 @@
 from jax.sharding import PartitionSpec as P
 
 KB = 16
+
+
+def exchange_directly(array, axis, split, join):
+    ways, here = (lax.axis_size(axis), lax.axis_index(axis))
+    width = array.shape[split] // ways
+    turned = jnp.roll(array, -here * width, axis=split)
+    got = [lax.slice_in_dim(turned, 0, width, axis=split)]
+    for far in range(1, ways):
+        sent = lax.slice_in_dim(turned, far * width, (far + 1) * width, axis=split)
+        got.append(lax.ppermute(sent, axis, [(d, (d + far) % ways) for d in range(ways)]))
+    line = jnp.concatenate(got[::-1], axis=join)
+    return jnp.roll(line, (here + 1) * got[0].shape[join], axis=join)
 
 
 def with_halo(block, sides, width):
@@ -118,7 +130,7 @@
     mine_blk = lax.axis_index("blk")
     share = KB // lax.axis_size("rows")
     moved, moved_wts = (
-        lax.all_to_all(buckets, "rows", split_axis=0, concat_axis=1, tiled=True),
+        exchange_directly(buckets, "rows", 0, 1),
         lax.all_to_all(bucket_wts, "rows", split_axis=0, concat_axis=1, tiled=True),
     )
     base = mine_blk * KB + lax.axis_index("rows") * share

time: 141 us -> 131 us (0.929)
  waiting for transfers between devices: 86 us -> 75.9 us
    all_to_all x1 -> x0, waiting for transfers between devices: 21.2 us -> none  [on_device(): lax.all_to_all(buckets, 'rows', split_axis=0, concat_axis=1, tiled=True)]
    all_to_all x1, waiting for transfers between devices: 0.38 us -> 16 us  [on_device(): lax.all_to_all(bucket_wts, 'rows', split_axis=0, concat_axis=1, tiled=True)]
    all_to_all x1 -> x0, starting transfers between devices: 4.27 us -> none  [on_device(): lax.all_to_all(buckets, 'rows', split_axis=0, concat_axis=1, tiled=True)]
    ppermute x0 -> x3, starting transfers between devices: none -> 3.93 us  [exchange_directly(): lax.ppermute(sent, axis, [(d, (d + far) % ways) for d in range(ways)])]
    all_to_all x1, waiting for transfers between devices: 1.91 us -> 0.01 us  [on_device(): lax.all_to_all(packed_wts, 'blk', split_axis=0, concat_axis=0, tiled=True)]
    unnamed x8 -> x19, local copies, waits for them, and re-layouts: 5.87 us -> 4.85 us
  transfers between devices with their start and end apart: 7 -> 9, of which waited for: 7 -> 5; matrix products, arithmetic and copies ran while one was open for 8% -> 9% of each run, Pallas kernels for 0% -> 0%
where the time goes in v1:
time: 131 us; the launch traced here: 130 us
  waiting for transfers between devices  75.9 us (58%)
  starting transfers between devices  27.7 us (21%)
  local copies, waits for them, and re-layouts  11.2 us (9%)
  matrix products  9.47 us (7%)
  other arithmetic  4.94 us (4%)
    all_to_all x1, waiting for transfers between devices, on_device(): lax.all_to_all(packed, 'blk', split_axis=0, concat_axis=0, tiled=True)  42.2 us
    all_to_all x1, waiting for transfers between devices, on_device(): lax.all_to_all(bucket_wts, 'rows', split_axis=0, concat_axis=1, tiled=True)  16 us
    ppermute x1, waiting for transfers between devices, with_halo(): lax.ppermute(lax.slice_in_dim(block, block.shape[dim] - width, None, axis...  15.2 us
    dot_general x6, matrix products, band_terms(): lax.dot_general(left, right, (((1,), (1,)), ((0,), (0,))), preferred_elem...  6.49 us
    all_to_all x1, starting transfers between devices, on_device(): lax.all_to_all(packed_ids, 'blk', split_axis=0, concat_axis=0, tiled=True)  5.78 us
    all_to_all x1, starting transfers between devices, on_device(): lax.all_to_all(packed, 'blk', split_axis=0, concat_axis=0, tiled=True)  5.03 us
    unnamed x19, local copies, waits for them, and re-layouts  4.85 us
    all_to_all x1, starting transfers between devices, on_device(): lax.all_to_all(packed_wts, 'blk', split_axis=0, concat_axis=0, tiled=True)  4.54 us
  transfers between devices with their start and end apart: 9, of which 5 were waited for; matrix products, arithmetic and copies ran while one was open for 9% of the time, Pallas kernels for 0%

profile of v1, /device:TPU:3, one launch (start us, length us, event | category | flops | bytes accessed | tf_op | source)
XLA Modules:
  0.0 129.5 jit_solution(14508968408892559565)
XLA Ops:
  0.0 0.7 and_select_fusion.1
  0.7 0.7 fusion.57
  1.5 0.7 multiply_add_fusion
  2.2 0.8 fusion.10
  3.0 0.7 all_to_all.31
  3.6 5.8 %all-to-all-start = ((bf16[8,4,1]{1,2,0:T(2,128)(2,1)}), bf16[8,4,1]{1,2,0:T(2,128)(2,1)S(1)}, u32[]{:S(2)}, u32[]{:S(2)}) async-start(bf16[8,4,1]{1,2,0:T(2,128)(2,1)} %all_to_all.31), calls=%async_computation | async-start | bytes 8192 | tf_op jit(solution)/shard_map/all_to_all | solution.py:111
  9.4 1.4 %copy.15 = bf16[2,8,120,256]{3,1,2,0:T(8,128)(2,1)S(1)} copy(bf16[2,8,120,256]{3,2,1,0:T(8,128)(2,1)} %bitcast.113) | data formatting | bytes 1966080
  10.8 0.6 convolution_convert_fusion.1
  11.5 1.7 %copy.16 = bf16[4,8,120,256]{3,2,1,0:T(8,128)(2,1)} copy(bf16[4,8,120,256]{3,1,2,0:T(8,128)(2,1)S(1)} %bitcast.103) | data formatting | bytes 3932160
  13.6 5.0 %all-to-all-start.1 = ((bf16[32,3,40,256]{3,2,1,0:T(8,128)(2,1)}), bf16[32,3,40,256]{3,2,1,0:T(8,128)(2,1)S(1)}, u32[]{:S(2)}, u32[]{:S(2)}) async-start(bf16[32,3,40,256]{3,2,1,0:T(8,128)(2,1)} %bitcast.101), calls=%async_computation.1 | async-start | bytes 3932160 | tf_op jit(solution)/shard_map/all_to_all | solution.py:109
  19.2 0.7 and_reduce_fusion
  20.0 0.8 convolution_convert_fusion.3
  21.1 42.2 %all-to-all-done.1 = bf16[32,3,40,256]{3,2,1,0:T(8,128)(2,1)S(1)} async-done(((bf16[32,3,40,256]{3,2,1,0:T(8,128)(2,1)}), bf16[32,3,40,256]{3,2,1,0:T(8,128)(2,1)S(1)}, u32[]{:S(2)}, u32[]{:S(2)}) %all-to-all-start.1) | async-done | bytes 1966112 | tf_op jit(solution)/shard_map/all_to_all | solution.py:109
  63.3 4.5 %all-to-all-start.2 = ((bf16[8,4,40]{2,1,0:T(4,128)(2,1)}), bf16[8,4,40]{2,1,0:T(4,128)(2,1)S(1)}, u32[]{:S(2)}, u32[]{:S(2)}) async-start(bf16[8,4,40]{2,1,0:T(4,128)(2,1)} %bitcast.4), calls=%async_computation.2 | async-start | bytes 16384 | tf_op jit(solution)/shard_map/all_to_all | solution.py:110
  68.2 0.7 convolution_convert_fusion
  69.3 0.7 fusion
  70.0 1.1 fusion.38
  71.2 1.1 collective-permute-start
  72.2 1.2 collective-permute-start.1
  73.6 0.7 reshape.492
  74.3 3.7 %all-to-all-start.3 = ((bf16[4,2,160]{2,1,0:T(2,128)(2,1)}), bf16[4,2,160]{2,1,0:T(2,128)(2,1)S(1)}, u32[]{:S(2)}, u32[]{:S(2)}) async-start(bf16[4,2,160]{2,1,0:T(2,128)(2,1)} %reshape.492), calls=%async_computation.3 | async-start | bytes 8192 | tf_op jit(solution)/shard_map/all_to_all | solution.py:134
  77.9 1.6 %collective-permute-start.2 = (bf16[4,2,3,40,256]{4,3,2,1,0:T(8,128)(2,1)}, bf16[4,2,3,40,256]{4,3,2,1,0:T(8,128)(2,1)S(1)}, u32[]{:S(2)}, u32[]{:S(2)}) collective-permute-start(bf16[4,2,3,40,256]{4,3,2,1,0:T(8,128)(2,1)} %get-tuple-element.109), channel_id=1, source_target_pairs={{0,1},{1,2},{2,3},{3,0},{4,5},{5,6},{6,7},{7,4},{8,9},{9,10},{10,1... | collective-permute-start | bytes 1474568 | tf_op jit(solution)/shard_map/ppermute | solution.py:16
  80.2 16.0 %all-to-all-done.3 = bf16[4,2,160]{2,1,0:T(2,128)(2,1)S(1)} async-done(((bf16[4,2,160]{2,1,0:T(2,128)(2,1)}), bf16[4,2,160]{2,1,0:T(2,128)(2,1)S(1)}, u32[]{:S(2)}, u32[]{:S(2)}) %all-to-all-start.3) | async-done | bytes 2592 | tf_op jit(solution)/shard_map/all_to_all | solution.py:134
  98.7 1.7 %fusion.2 = f32[6,3,256,256]{3,2,0,1:T(8,128)S(1)} fusion(f32[6,3,256,256]{3,2,0,1:T(8,128)S(1)} %scatter-add.26, s32[]{:T(128)} %bitcast.13, s32[]{:T(128)} %bitcast.14, bf16[4,320,256]{2,1,0:T(8,128)(2,1)S(1)} %bitcast.95, bf16[4,320,256]{2,1,0:T(8,128)(2,1)S(1)} %bitcast.106, f32[4,1,256,256]{3,2,0,1:T(8,128)S(1)} %convolution_bitcast_fusion.5), kind=kOutput, calls=%fused_computation.16 | convolution fusion | flops 168034304 | bytes 3407880 | tf_op jit(solution)/shard_map/dot_general | solution.py:62
  100.4 2.4 %fusion.9 = f32[6,3,256,256]{3,2,0,1:T(8,128)S(1)} fusion(f32[6,3,256,256]{3,2,0,1:T(8,128)S(1)} %fusion.2, s32[]{:T(128)} %bitcast.17, s32[]{:T(128)} %bitcast.18, bf16[4,320,256]{2,1,0:T(8,128)(2,1)S(1)} %bitcast.96, bf16[4,320,256]{2,1,0:T(8,128)(2,1)S(1)} %bitcast.97, pred[]{:T(512)} %and_reduce_fusion), kind=kOutput, calls=%fused_computation.23 | convolution fusion | flops 168296448 | bytes 3407881 | tf_op jit(solution)/shard_map/dot_general | solution.py:62
  102.9 0.6 fusion.4
  103.5 0.6 fusion.6
  104.9 2.8 %collective-permute-start.3 = (f32[1,3,256,256]{3,2,0,1:T(8,128)S(1)}, f32[1,3,256,256]{3,2,0,1:T(8,128)S(1)}, u32[]{:S(2)}, u32[]{:S(2)}) collective-permute-start(f32[1,3,256,256]{3,2,0,1:T(8,128)S(1)} %get-tuple-element.102), channel_id=1, source_target_pairs={{0,1},{1,2},{2,3},{3,4},{4,5},{5,6},{6,7},{7,8},{8,9},{9,10},{10,1... | collective-permute-start | bytes 2359304 | tf_op jit(solution)/shard_map/ppermute | solution.py:26
  107.8 1.9 %collective-permute-start.4 = (f32[1,3,256,256]{3,2,0,1:T(8,128)S(1)}, f32[1,3,256,256]{3,2,0,1:T(8,128)S(1)}, u32[]{:S(2)}, u32[]{:S(2)}) collective-permute-start(f32[1,3,256,256]{3,2,0,1:T(8,128)S(1)} %get-tuple-element.101), channel_id=1, source_target_pairs={{1,0},{2,1},{3,2},{4,3},{5,4},{6,5},{7,6},{8,7},{9,8},{10,9},{11,1... | collective-permute-start | bytes 2359304 | tf_op jit(solution)/shard_map/ppermute | solution.py:29
  109.9 15.2 %collective-permute-done.3 = f32[1,3,256,256]{3,2,0,1:T(8,128)S(1)} collective-permute-done((f32[1,3,256,256]{3,2,0,1:T(8,128)S(1)}, f32[1,3,256,256]{3,2,0,1:T(8,128)S(1)}, u32[]{:S(2)}, u32[]{:S(2)}) %collective-permute-start.3) | collective-permute-done | bytes 786464 | tf_op jit(solution)/shard_map/ppermute | solution.py:26
  125.2 2.1 %collective-permute-done.4 = f32[1,3,256,256]{3,2,0,1:T(8,128)S(1)} collective-permute-done((f32[1,3,256,256]{3,2,0,1:T(8,128)S(1)}, f32[1,3,256,256]{3,2,0,1:T(8,128)S(1)}, u32[]{:S(2)}, u32[]{:S(2)}) %collective-permute-start.4) | collective-permute-done | bytes 786464 | tf_op jit(solution)/shard_map/ppermute | solution.py:29
  127.5 2.1 %copy.14 = f32[4,3,256,256]{3,2,1,0:T(8,128)} copy(f32[4,3,256,256]{3,2,0,1:T(8,128)S(1)} %fusion.11) | data formatting | bytes 6291456 | tf_op jit(solution)/shard_map/scatter-add | solution.py:77
  (47 shorter events, 6.8 us)
Async XLA Ops:
  3.6 9.9 %all-to-all-start = ((bf16[8,4,1]{1,2,0:T(2,128)(2,1)}), bf16[8,4,1]{1,2,0:T(2,128)(2,1)S(1)}, u32[]{:S(2)}, u32[]{:S(2)}) async-start(bf16[8,4,1]{1,2,0:T(2,128)(2,1)} %all_to_all.31), calls=%async_computation | async-start | bytes 8192 | tf_op jit(solution)/shard_map/all_to_all | solution.py:111
  11.5 7.7 %copy-start = (s32[4]{0:T(128)S(1)}, s32[4]{0:T(128)}, u32[]{:S(2)}) copy-start(s32[4]{0:T(128)} %constant.309.clone.1) | copy-start | bytes 52
  11.5 8.5 %copy-start.1 = (bf16[16,40]{1,0:T(8,128)(2,1)S(1)}, bf16[16,40]{1,0:T(8,128)(2,1)}, u32[]{:S(2)}) copy-start(bf16[16,40]{1,0:T(8,128)(2,1)} %param.23) | copy-start | bytes 3844
  11.5 8.5 %copy-start.2 = (s32[16]{0:T(128)S(1)}, s32[16]{0:T(128)}, u32[]{:S(2)}) copy-start(s32[16]{0:T(128)} %param.21) | copy-start | bytes 196
  13.6 49.7 %all-to-all-start.1 = ((bf16[32,3,40,256]{3,2,1,0:T(8,128)(2,1)}), bf16[32,3,40,256]{3,2,1,0:T(8,128)(2,1)S(1)}, u32[]{:S(2)}, u32[]{:S(2)}) async-start(bf16[32,3,40,256]{3,2,1,0:T(8,128)(2,1)} %bitcast.101), calls=%async_computation.1 | async-start | bytes 3932160 | tf_op jit(solution)/shard_map/all_to_all | solution.py:109
  63.3 10.1 %all-to-all-start.2 = ((bf16[8,4,40]{2,1,0:T(4,128)(2,1)}), bf16[8,4,40]{2,1,0:T(4,128)(2,1)S(1)}, u32[]{:S(2)}, u32[]{:S(2)}) async-start(bf16[8,4,40]{2,1,0:T(4,128)(2,1)} %bitcast.4), calls=%async_computation.2 | async-start | bytes 16384 | tf_op jit(solution)/shard_map/all_to_all | solution.py:110
  71.2 25.1 %collective-permute-start = (bf16[4,2,3,40,256]{4,3,2,1,0:T(8,128)(2,1)}, bf16[4,2,3,40,256]{4,3,2,1,0:T(8,128)(2,1)S(1)}, u32[]{:S(2)}, u32[]{:S(2)}) collective-permute-start(bf16[4,2,3,40,256]{4,3,2,1,0:T(8,128)(2,1)} %get-tuple-element.111), channel_id=1, source_target_pairs={{0,3},{1,0},{2,1},{3,2},{4,7},{5,4},{6,5},{7,6},{8,11},{9,8},{10,9... | collective-permute-start | bytes 1474568 | tf_op jit(solution)/shard_map/ppermute | solution.py:16
  72.2 24.1 %collective-permute-start.1 = (bf16[4,2,3,40,256]{4,3,2,1,0:T(8,128)(2,1)}, bf16[4,2,3,40,256]{4,3,2,1,0:T(8,128)(2,1)S(1)}, u32[]{:S(2)}, u32[]{:S(2)}) collective-permute-start(bf16[4,2,3,40,256]{4,3,2,1,0:T(8,128)(2,1)} %get-tuple-element.110), channel_id=1, source_target_pairs={{0,2},{1,3},{2,0},{3,1},{4,6},{5,7},{6,4},{7,5},{8,10},{9,11},{10,... | collective-permute-start | bytes 1474568 | tf_op jit(solution)/shard_map/ppermute | solution.py:16
  74.3 21.9 %all-to-all-start.3 = ((bf16[4,2,160]{2,1,0:T(2,128)(2,1)}), bf16[4,2,160]{2,1,0:T(2,128)(2,1)S(1)}, u32[]{:S(2)}, u32[]{:S(2)}) async-start(bf16[4,2,160]{2,1,0:T(2,128)(2,1)} %reshape.492), calls=%async_computation.3 | async-start | bytes 8192 | tf_op jit(solution)/shard_map/all_to_all | solution.py:134
  77.9 18.4 %collective-permute-start.2 = (bf16[4,2,3,40,256]{4,3,2,1,0:T(8,128)(2,1)}, bf16[4,2,3,40,256]{4,3,2,1,0:T(8,128)(2,1)S(1)}, u32[]{:S(2)}, u32[]{:S(2)}) collective-permute-start(bf16[4,2,3,40,256]{4,3,2,1,0:T(8,128)(2,1)} %get-tuple-element.109), channel_id=1, source_target_pairs={{0,1},{1,2},{2,3},{3,0},{4,5},{5,6},{6,7},{7,4},{8,9},{9,10},{10,1... | collective-permute-start | bytes 1474568 | tf_op jit(solution)/shard_map/ppermute | solution.py:16
  104.9 20.2 %collective-permute-start.3 = (f32[1,3,256,256]{3,2,0,1:T(8,128)S(1)}, f32[1,3,256,256]{3,2,0,1:T(8,128)S(1)}, u32[]{:S(2)}, u32[]{:S(2)}) collective-permute-start(f32[1,3,256,256]{3,2,0,1:T(8,128)S(1)} %get-tuple-element.102), channel_id=1, source_target_pairs={{0,1},{1,2},{2,3},{3,4},{4,5},{5,6},{6,7},{7,8},{8,9},{9,10},{10,1... | collective-permute-start | bytes 2359304 | tf_op jit(solution)/shard_map/ppermute | solution.py:26
  107.8 19.5 %collective-permute-start.4 = (f32[1,3,256,256]{3,2,0,1:T(8,128)S(1)}, f32[1,3,256,256]{3,2,0,1:T(8,128)S(1)}, u32[]{:S(2)}, u32[]{:S(2)}) collective-permute-start(f32[1,3,256,256]{3,2,0,1:T(8,128)S(1)} %get-tuple-element.101), channel_id=1, source_target_pairs={{1,0},{2,1},{3,2},{4,3},{5,4},{6,5},{7,6},{8,7},{9,8},{10,9},{11,1... | collective-permute-start | bytes 2359304 | tf_op jit(solution)/shard_map/ppermute | solution.py:29
